TPU v7x, 32 devices: a whole 2x2x4 slice. The times are simulated.
32 devices in a mesh: ep: 8 (over y, x, core), tp: 4 (over z).
Axes of the slice: x: 2, y: 2, z: 4, core: 2. Of those that a mesh axis runs over, the one named last changes fastest.
Arguments:
- tokens: bfloat16 [2048, 7168], P('ep', 'tp'), may hold values from -78 to 78
- norm_gain: bfloat16 [7168], P('tp'), may hold values from 0.5 to 1.5
- expert_ids: int32 [2048, 8], P('ep'), may hold values from 0 to 63, all different within a row
- gate_prob: bfloat16 [2048, 8], P('ep'), may hold values from 0.049804688 to 1
- w_gate: bfloat16 [8, 7168, 2048], P('ep', None, 'tp'), may hold values from -0.0625 to 0.0625
- w_up: bfloat16 [8, 7168, 2048], P('ep', None, 'tp'), may hold values from -0.0625 to 0.0625
- w_down: bfloat16 [8, 2048, 7168], P('ep', 'tp'), may hold values from -0.125 to 0.125
Outputs:
- combined: bfloat16 [2048, 7168], P('ep', 'tp')
Inputs may be any that keep to these rules, and one draw needn't show every extreme that they name: `expert_ids`: each row names 8 different experts.
All inputs are finite; a program needn't handle non-finite values.
Results may differ from a plain program's by a relative error of at most 0.01.
Values may be sent and summed in bfloat16 or wider, within the bound.
A program may use at most 128 MiB of HBM per device.

v0:
```python
import functools

import jax
import jax.numpy as jnp
from jax import lax
from jax.experimental import pallas as pl
from jax.experimental.pallas import tpu as pltpu
from jax.sharding import PartitionSpec as P

TOP = 8
EXP_DEV = 8
SHARE = 7
EPSILON = 1e-06
BF16 = jnp.bfloat16
F32 = jnp.float32


def look_up(table, index):
    span = len(table) ** 2
    total = 0
    for i, value in enumerate(table):
        if value:
            total = total + value * (1 - ((index - i) * (index - i) + span - 1) // span)
    return total


def near_first(n_tp):
    table = []
    for z in range(n_tp):
        inner = 1 if z < n_tp / 2 else -1
        table += sorted(range(n_tp), key=lambda s: (abs(s - z), -inner * (s - z)))
    return table


def body(
    n_ep, n_tp, rows, width, cap, wide, n_tok, n_slot,
    tok_hbm, gain_ref, ids_ref, prob_ref, gate_hbm, up_hbm, down_hbm,
    out_ref,
    tok, gains, stats, scale, dmat, wmat, send, recv, slot_in, w_gate, w_up, w_down,
    acc, hid, ret, ret_slot, in_tok, in_slot, part,
    load_sem, st_send, st_recv, zt_send, zt_recv, xs, xr, ys, yr, zp_send, zp_recv,
):
    e, z = lax.axis_index("ep"), lax.axis_index("tp")
    last = n_tp - 1
    items = n_tok + n_slot
    slots = n_ep * cap
    steps = n_tp * n_tok
    table = near_first(n_tp)

    def nth(k):
        return look_up(table, z * n_tp + k)

    def column(slice_index, item):
        return pl.multiple_of(slice_index * width + item * wide, wide)

    def remote(axis, index, src, dst, send_sem, recv_sem):
        return pltpu.make_async_remote_copy(
            src_ref=src,
            dst_ref=dst,
            send_sem=send_sem,
            recv_sem=recv_sem,
            device_id={axis: index},
            device_id_type=pl.DeviceIdType.MESH,
        )

    def each_peer(fn):
        def step(shift, carry):
            fn(lax.rem(e + shift, n_ep))
            return carry

        lax.fori_loop(1, n_ep, step, 0)

    loads = [
        pltpu.make_async_copy(
            tok_hbm.at[:, pl.ds(m * wide, wide)], tok.at[z, m], load_sem.at[m]
        )
        for m in range(items)
    ]
    weights = [
        pltpu.make_async_copy(src, dst, load_sem.at[items + i])
        for i, (src, dst) in enumerate(
            ((gate_hbm, w_gate), (up_hbm, w_up), (down_hbm, w_down))
        )
    ]
    for copy in loads + weights:
        copy.start()

    barrier = pltpu.get_barrier_semaphore()

    def greet(axis, index):
        pl.semaphore_signal(
            barrier, inc=1, device_id={axis: index}, device_id_type=pl.DeviceIdType.MESH
        )

    each_peer(lambda p: greet("ep", p))
    for shift in range(1, n_tp):
        greet("tp", lax.rem(z + shift, n_tp))

    ids = ids_ref[...]
    prob = prob_ref[...].astype(F32)
    lane = lax.broadcasted_iota(jnp.int32, (rows, 128), 1)
    picked = jnp.zeros((rows, 128), F32)
    chance = jnp.zeros((rows, 128), F32)
    for k in range(TOP):
        same = ids[:, k : k + 1] == lane
        picked = jnp.where(same, 1.0, picked)
        chance = jnp.where(same, prob[:, k : k + 1], chance)
    picked = picked.astype(BF16)
    earlier = (
        lax.broadcasted_iota(jnp.int32, (rows, rows), 1)
        < lax.broadcasted_iota(jnp.int32, (rows, rows), 0)
    )
    earlier = jnp.where(earlier, 1.0, 0.0).astype(BF16)
    before = jnp.dot(earlier, picked, preferred_element_type=F32).astype(BF16)
    spread_row = lax.broadcasted_iota(jnp.int32, (128, slots), 0)
    spread_col = lax.broadcasted_iota(jnp.int32, (128, slots), 1)
    spread = jnp.where(
        (spread_col >= spread_row * cap) & (spread_col < (spread_row + 1) * cap), 1.0, 0.0
    ).astype(BF16)
    is_picked = jnp.dot(picked, spread, preferred_element_type=F32)
    place = jnp.dot(before, spread, preferred_element_type=F32)
    weight = jnp.dot(chance.astype(BF16), spread, preferred_element_type=F32)
    position = lax.rem(lax.broadcasted_iota(jnp.int32, (rows, slots), 1), cap).astype(F32)
    hit = (is_picked > 0.5) & (place == position)
    wmat[...] = jnp.where(hit, weight, 0.0).astype(BF16)
    dmat[...] = jnp.where(hit, 1.0, 0.0).T.astype(BF16)

    square = jnp.zeros((rows, 1), F32)
    for m in range(items):
        loads[m].wait()
        values = tok[z, m].astype(F32)
        square = square + jnp.sum(values * values, axis=1, keepdims=True)
    stats[z] = jnp.broadcast_to(square, (rows, 128)).T[0:8, :]
    gains[z] = gain_ref[...]

    pl.semaphore_wait(barrier, n_ep - 1 + n_tp - 1)

    def share(shift):
        peer = lax.rem(z + shift, n_tp)
        return (
            remote("tp", peer, stats.at[z], stats.at[z], st_send.at[shift, 0], st_recv.at[shift, 0]),
            remote("tp", peer, gains.at[z], gains.at[z], st_send.at[shift, 1], st_recv.at[shift, 1]),
        )

    for shift in range(1, n_tp):
        for copy in share(shift):
            copy.start()

    def along(way, s, m, ref):
        peer = lax.rem(z + n_tp - 1 if way == 0 else z + 1, n_tp)
        return remote("tp", peer, ref, ref, zt_send.at[way, s, m], zt_recv.at[s, m])

    for m in range(n_tok):
        @pl.when(z > 0)
        def _():
            along(0, z, m, tok.at[z, m]).start()

        @pl.when(z < last)
        def _():
            along(1, z, m, tok.at[z, m]).start()

    for shift in range(1, n_tp):
        for copy in share(shift):
            copy.wait_recv()
    total = stats[0]
    for i in range(1, n_tp):
        total = total + stats[i]
    factor = lax.rsqrt(total / (width * n_tp) + EPSILON)
    scale[...] = jnp.broadcast_to(factor[0:1, :], (128, rows)).T

    def to_peers(index, dst, send_sem, recv_sem):
        own = pl.ds(pl.multiple_of(e * cap, cap), cap)
        dst[own, :] = send[index, own, :]

        def one(p):
            theirs = pl.ds(pl.multiple_of(p * cap, cap), cap)
            remote("ep", p, send.at[index, theirs, :], dst.at[own, :], send_sem, recv_sem).start()

        each_peer(one)

    def all_peers(index, dst, send_sem, recv_sem):
        most = pl.ds(0, (n_ep - 1) * cap)
        return remote(
            "ep", lax.rem(e + 1, n_ep), send.at[index, most, :], dst.at[most, :], send_sem, recv_sem
        )

    def dispatch(s, m, index, dst):
        gain = gains[s, :, pl.ds(pl.multiple_of(m * wide, wide), wide)]
        normed = tok[s, m].astype(F32) * scale[:, 0:1] * gain
        placed = jnp.dot(dmat[...], normed.astype(BF16), preferred_element_type=F32)
        send[index] = placed.astype(BF16)
        to_peers(index, dst, xs.at[index], xr.at[index])

    def gate_up(chunk, row, first=False):
        values = chunk[...]
        at = pl.ds(row, wide)
        for i, matrix in enumerate((w_gate, w_up)):
            product = jnp.dot(values, matrix[at, :], preferred_element_type=F32)
            acc[i] = product if first else acc[i] + product

    for a in range(n_slot):
        dispatch(z, n_tok + a, steps + a, slot_in.at[z, a])

    @pl.loop(0, n_tok)
    def _(j):
        dispatch(z, j, j, recv.at[j])

    weights[0].wait()
    weights[1].wait()
    for a in range(n_slot):
        all_peers(steps + a, slot_in.at[z, a], xs.at[steps + a], xr.at[steps + a]).wait_recv()

        @pl.when(z > 0)
        def _():
            along(0, z, n_tok + a, slot_in.at[z, a]).start()

        @pl.when(z < last)
        def _():
            along(1, z, n_tok + a, slot_in.at[z, a]).start()

        gate_up(slot_in.at[z, a], column(z, n_tok + a), first=a == 0)

    def arrive(k, m, ref_of):
        @pl.when(z + k <= last)
        def _():
            along(0, z + k, m, ref_of(z + k)).wait_recv()

            @pl.when(z > 0)
            def _():
                along(0, z + k, m, ref_of(z + k)).start()

        @pl.when(z - k >= 0)
        def _():
            along(1, z - k, m, ref_of(z - k)).wait_recv()

            @pl.when(z < last)
            def _():
                along(1, z - k, m, ref_of(z - k)).start()

    def take_in(index, s, m):
        all_peers(index, recv.at[index], xs.at[index], xr.at[index]).wait_recv()
        gate_up(recv.at[index], column(s, m))

    @pl.loop(n_tok, steps)
    def _(i):
        k, j = i // n_tok, i % n_tok
        arrive(k, j, lambda s: tok.at[s, j])
        dispatch(nth(k), j, i, recv.at[i])
        take_in(i - n_tok, nth(k - 1), j)
        for a in range(n_slot):
            @pl.when((j == n_tok - 1) & (k < last))
            def _():
                arrive(k, n_tok + a, lambda s: slot_in.at[s, a])

    for a in range(n_slot):
        @pl.loop(1, last)
        def _(k):
            s = nth(k)
            gate_up(slot_in.at[s, a], column(s, n_tok + a))

    @pl.loop(0, n_tok)
    def _(j):
        take_in(steps - n_tok + j, nth(last), j)

    for a in range(n_slot):
        arrive(last, n_tok + a, lambda s: slot_in.at[s, a])
        s = nth(last)
        gate_up(slot_in.at[s, a], column(s, n_tok + a))

    gate_act = acc[0]
    hid[...] = (gate_act / (1.0 + jnp.exp(-gate_act)) * acc[1]).astype(BF16)
    weights[2].wait()

    def down(index, s, m):
        matrix = w_down[:, pl.ds(column(s, m), wide)]
        send[index] = jnp.dot(hid[...], matrix, preferred_element_type=F32).astype(BF16)

    def onward(way, k, s, m, src, landing):
        peer = lax.rem(z + 1 if way == 0 else z + n_tp - 1, n_tp)
        return remote("tp", peer, src, landing.at[way, s], zp_send.at[k, m], zp_recv.at[way, s, m])

    for a in range(n_slot):
        all_peers(steps + a, slot_in.at[z, a], xs.at[steps + a], xr.at[steps + a]).wait_send()

    def far(k):
        return nth(last - k)

    for a in range(n_slot):
        @pl.loop(0, n_tp)
        def _(k):
            s, index = far(k), steps + k * n_slot + a
            down(index, s, n_tok + a)

            @pl.when((z == 0) & (k < last))
            def _():
                onward(0, k, s, n_tok + a, send.at[index], in_slot.at[a]).start()

            @pl.when((z == last) & (k < last))
            def _():
                onward(1, k, s, n_tok + a, send.at[index], in_slot.at[a]).start()

    @pl.loop(0, steps)
    def _(i):
        k, j = i // n_tok, i % n_tok
        all_peers(i, recv.at[i], xs.at[i], xr.at[i]).wait_send()
        down(i, far(k), j)
        to_peers(i, ret.at[i], ys.at[i], yr.at[i])

    for a in range(n_slot):
        @pl.loop(0, last)
        def _(k):
            s, index = far(k), steps + k * n_slot + a

            def pass_on(way):
                copy = onward(way, k, s, n_tok + a, send.at[index], in_slot.at[a])
                copy.wait_recv()
                summed = send[index].astype(F32) + in_slot[a, way, s].astype(F32)
                send[index] = summed.astype(BF16)
                copy.start()

            @pl.when((s > z) & (z > 0))
            def _():
                pass_on(0)

            @pl.when((s < z) & (z < last))
            def _():
                pass_on(1)

    def combine(i):
        all_peers(i, ret.at[i], ys.at[i], yr.at[i]).wait_recv()
        return jnp.dot(wmat[...], ret[i], preferred_element_type=F32)

    def add_in(way, s, j):
        landing = in_tok.at[j]
        onward(way, 0, s, j, landing.at[way, s], landing).wait_recv()
        part[...] = part[...] + in_tok[j, way, s].astype(F32)

    def forward_part(i):
        k, j = i // n_tok, i % n_tok
        s = far(k)
        part[...] = combine(i)

        @pl.when((s > z) & (z > 0))
        def _():
            add_in(0, s, j)

        @pl.when((s < z) & (z < last))
        def _():
            add_in(1, s, j)

        recv[i, 0:rows, :] = part[...].astype(BF16)

        @pl.when(s > z)
        def _():
            onward(0, k, s, j, recv.at[i, pl.ds(0, rows), :], in_tok.at[j]).start()

        @pl.when(s < z)
        def _():
            onward(1, k, s, j, recv.at[i, pl.ds(0, rows), :], in_tok.at[j]).start()

    @pl.loop(0, n_tok)
    def _(i):
        forward_part(i)

    for a in range(n_slot):
        index = steps + last * n_slot + a

        def add_slot(way):
            copy = onward(way, 0, z, n_tok + a, send.at[index], in_slot.at[a])
            copy.wait_recv()
            send[index] = (send[index].astype(F32) + in_slot[a, way, z].astype(F32)).astype(BF16)

        @pl.when(z > 0)
        def _():
            add_slot(0)

        @pl.when(z < last)
        def _():
            add_slot(1)

        to_peers(index, ret_slot.at[a], ys.at[steps + a], yr.at[steps + a])

    @pl.loop(n_tok, steps - n_tok)
    def _(i):
        forward_part(i)

    @pl.loop(0, n_tok)
    def _(j):
        part[...] = combine(steps - n_tok + j)

        @pl.when(z > 0)
        def _():
            add_in(0, z, j)

        @pl.when(z < last)
        def _():
            add_in(1, z, j)

        out_ref[:, pl.ds(pl.multiple_of(j * wide, wide), wide)] = part[...].astype(BF16)

    for a in range(n_slot):
        index = steps + last * n_slot + a
        all_peers(index, ret_slot.at[a], ys.at[steps + a], yr.at[steps + a]).wait_recv()
        m = n_tok + a
        out_ref[:, m * wide : (m + 1) * wide] = jnp.dot(
            wmat[...], ret_slot[a], preferred_element_type=F32
        ).astype(BF16)

    for shift in range(1, n_tp):
        for copy in share(shift):
            copy.wait_send()

    @pl.loop(0, n_tp)
    def _(s):
        @pl.when((z > 0) & (s >= z))
        def _():
            for m in range(items):
                ref = tok.at[s, m] if m < n_tok else slot_in.at[s, m - n_tok]
                along(0, s, m, ref).wait_send()

        @pl.when((z < last) & (s <= z))
        def _():
            for m in range(items):
                ref = tok.at[s, m] if m < n_tok else slot_in.at[s, m - n_tok]
                along(1, s, m, ref).wait_send()

    @pl.loop(0, steps)
    def _(i):
        all_peers(i, ret.at[i], ys.at[i], yr.at[i]).wait_send()

    for a in range(n_slot):
        index = steps + last * n_slot + a
        all_peers(index, ret_slot.at[a], ys.at[steps + a], yr.at[steps + a]).wait_send()

    @pl.loop(0, last)
    def _(k):
        for m in range(n_tok):
            onward(
                0, k, 0, m, recv.at[k * n_tok + m, pl.ds(0, rows), :], in_tok.at[m]
            ).wait_send()
        for a in range(n_slot):
            onward(
                0, k, 0, n_tok + a, send.at[steps + k * n_slot + a], in_slot.at[a]
            ).wait_send()


def local(tokens, norm_gain, expert_ids, gate_prob, w_gate, w_up, w_down):
    n_ep = lax.axis_size("ep")
    n_tp = lax.axis_size("tp")
    rows, width = tokens.shape
    cap = max(2, 2 * rows * TOP // (EXP_DEV * n_ep))
    slots = n_ep * cap
    wide = 256 if width % 256 == 0 else 128
    items = width // wide
    n_slot = max(1, items // SHARE)
    n_tok = items - n_slot
    units = w_gate.shape[2]
    steps = n_tp * n_tok

    kernel = functools.partial(body, n_ep, n_tp, rows, width, cap, wide, n_tok, n_slot)
    vmem = pl.BlockSpec(memory_space=pltpu.VMEM)
    hbm = pl.BlockSpec(memory_space=pl.ANY)
    dma = pltpu.SemaphoreType.DMA
    return pl.pallas_call(
        kernel,
        out_shape=jax.ShapeDtypeStruct((rows, width), BF16),
        in_specs=[hbm, vmem, vmem, vmem, hbm, hbm, hbm],
        out_specs=vmem,
        scratch_shapes=[
            pltpu.VMEM((n_tp, items, rows, wide), BF16),
            pltpu.VMEM((n_tp, 1, width), F32),
            pltpu.VMEM((n_tp, 8, rows), F32),
            pltpu.VMEM((rows, 128), F32),
            pltpu.VMEM((slots, rows), BF16),
            pltpu.VMEM((rows, slots), BF16),
            pltpu.VMEM((n_tp * items, slots, wide), BF16),
            pltpu.VMEM((steps, slots, wide), BF16),
            pltpu.VMEM((n_tp, n_slot, slots, wide), BF16),
            pltpu.VMEM((n_tp * width, units), BF16),
            pltpu.VMEM((n_tp * width, units), BF16),
            pltpu.VMEM((units, n_tp * width), BF16),
            pltpu.VMEM((2, slots, units), F32),
            pltpu.VMEM((slots, units), BF16),
            pltpu.VMEM((steps, slots, wide), BF16),
            pltpu.VMEM((n_slot, slots, wide), BF16),
            pltpu.VMEM((n_tok, 2, n_tp, rows, wide), BF16),
            pltpu.VMEM((n_slot, 2, n_tp, slots, wide), BF16),
            pltpu.VMEM((rows, wide), F32),
            dma((items + 3,)),
            dma((n_tp, 2)),
            dma((n_tp, 2)),
            dma((2, n_tp, items)),
            dma((n_tp, items)),
            dma((steps + n_slot,)),
            dma((steps + n_slot,)),
            dma((steps + n_slot,)),
            dma((steps + n_slot,)),
            dma((n_tp, items)),
            dma((2, n_tp, items)),
        ],
        compiler_params=pltpu.CompilerParams(
            collective_id=0, has_side_effects=True, vmem_limit_bytes=67043328
        ),
    )(
        tokens,
        norm_gain.astype(F32).reshape(1, width),
        expert_ids,
        gate_prob,
        w_gate[0],
        w_up[0],
        w_down[0],
    )


def solution(mesh):
    placed = (
        P("ep", "tp"),
        P("tp"),
        P("ep", None),
        P("ep", None),
        P("ep", None, "tp"),
        P("ep", None, "tp"),
        P("ep", "tp", None),
    )
    return jax.shard_map(
        local, mesh=mesh, in_specs=placed, out_specs=P("ep", "tp"), check_vma=False
    )
```

profile of v0, /device:TPU:1, one launch (start us, length us, event | category | flops | bytes accessed | tf_op | source)
XLA Modules:
  0.0 167.8 jit_solution(11510286205786297610)
XLA Ops:
  0.0 1.3 reshape.8.gain_ref
  1.3 1.4 copy.9.prob_ref
  2.7 1.5 copy.8.ids_ref
  4.2 161.4 %shard_map.73 = bf16[256,1792]{1,0:T(8,128)(2,1)} custom-call(bf16[256,1792]{1,0:T(8,128)(2,1)} %tok_hbm.1, f32[1,1792]{1,0:T(1,128)} %reshape.8.gain_ref, s32[256,8]{1,0:T(8,128)} %copy.8.ids_ref, bf16[256,8]{1,0:T(8,128)(2,1)} %copy.9.prob_ref, bf16[7168,512]{1,0:T(8,128)(2,1)} %bitcast.3, bf16[7168,512]{1,0:T(8,128)(2,1)} %bitcast.4, ...), custom_call_target="tpu_custom_call" | custom-call | tf_op jit(solution)/shard_map/pallas_call | solution.py:464
  165.6 2.2 %copy.11 = bf16[256,1792]{1,0:T(8,128)(2,1)} copy(bf16[256,1792]{1,0:T(8,128)(2,1)} %shard_map.73) | data formatting | bytes 1835008
where the time goes:
time: 168 us
  Pallas kernels  161 us (96%)
  local copies, waits for them, and re-layouts  6.34 us (4%)
    pallas_call x1, Pallas kernels, local(): pl.pallas_call(kernel, out_shape=jax.ShapeDtypeStruct((rows, width), BF16...  161 us
    unnamed x3, local copies, waits for them, and re-layouts  5.06 us

commit v1 on v0

--- a/solution.py
+++ b/solution.py
@@ -36,9 +36,9 @@
     n_ep, n_tp, rows, width, cap, wide, n_tok, n_slot,
     tok_hbm, gain_ref, ids_ref, prob_ref, gate_hbm, up_hbm, down_hbm,
     out_ref,
-    tok, gains, stats, scale, dmat, wmat, send, recv, slot_in, w_gate, w_up, w_down,
+    tok, stats, rowscale, turned, slotscale, dmat, wmat, send, recv, slot_in, w_gate, w_up, w_down,
     acc, hid, ret, ret_slot, in_tok, in_slot, part,
-    load_sem, st_send, st_recv, zt_send, zt_recv, xs, xr, ys, yr, zp_send, zp_recv,
+    load_sem, st_send, st_recv, sc_send, sc_recv, zt_send, zt_recv, xs, xr, ys, yr, zp_send, zp_recv,
 ):
     e, z = lax.axis_index("ep"), lax.axis_index("tp")
     last = n_tp - 1
@@ -96,8 +96,8 @@
     for shift in range(1, n_tp):
         greet("tp", lax.rem(z + shift, n_tp))
 
-    ids = ids_ref[...]
-    prob = prob_ref[...].astype(F32)
+    ids = ids_ref[...].T
+    prob = prob_ref[...].astype(F32).T
     lane = lax.broadcasted_iota(jnp.int32, (rows, 128), 1)
     picked = jnp.zeros((rows, 128), F32)
     chance = jnp.zeros((rows, 128), F32)
@@ -125,48 +125,37 @@
     wmat[...] = jnp.where(hit, weight, 0.0).astype(BF16)
     dmat[...] = jnp.where(hit, 1.0, 0.0).T.astype(BF16)
 
-    square = jnp.zeros((rows, 1), F32)
+    pl.semaphore_wait(barrier, n_ep - 1 + n_tp - 1)
+
+    def along(way, s, m, ref):
+        peer = lax.rem(z + n_tp - 1 if way == 0 else z + 1, n_tp)
+        return remote("tp", peer, ref, ref, zt_send.at[way, s, m], zt_recv.at[s, m])
+
+    square = jnp.zeros((rows, wide), F32)
+    gain = gain_ref[...].astype(F32).reshape(1, width)
     for m in range(items):
         loads[m].wait()
         values = tok[z, m].astype(F32)
-        square = square + jnp.sum(values * values, axis=1, keepdims=True)
+        square = square + values * values
+        tok[z, m] = (values * gain[:, m * wide : (m + 1) * wide]).astype(BF16)
+        if m < n_tok:
+            @pl.when(z > 0)
+            def _():
+                along(0, z, m, tok.at[z, m]).start()
+
+            @pl.when(z < last)
+            def _():
+                along(1, z, m, tok.at[z, m]).start()
+
+    square = jnp.sum(square, axis=1, keepdims=True)
     stats[z] = jnp.broadcast_to(square, (rows, 128)).T[0:8, :]
-    gains[z] = gain_ref[...]
-
-    pl.semaphore_wait(barrier, n_ep - 1 + n_tp - 1)
 
     def share(shift):
         peer = lax.rem(z + shift, n_tp)
-        return (
-            remote("tp", peer, stats.at[z], stats.at[z], st_send.at[shift, 0], st_recv.at[shift, 0]),
-            remote("tp", peer, gains.at[z], gains.at[z], st_send.at[shift, 1], st_recv.at[shift, 1]),
-        )
+        return remote("tp", peer, stats.at[z], stats.at[z], st_send.at[shift], st_recv.at[shift])
 
     for shift in range(1, n_tp):
-        for copy in share(shift):
-            copy.start()
-
-    def along(way, s, m, ref):
-        peer = lax.rem(z + n_tp - 1 if way == 0 else z + 1, n_tp)
-        return remote("tp", peer, ref, ref, zt_send.at[way, s, m], zt_recv.at[s, m])
-
-    for m in range(n_tok):
-        @pl.when(z > 0)
-        def _():
-            along(0, z, m, tok.at[z, m]).start()
-
-        @pl.when(z < last)
-        def _():
-            along(1, z, m, tok.at[z, m]).start()
-
-    for shift in range(1, n_tp):
-        for copy in share(shift):
-            copy.wait_recv()
-    total = stats[0]
-    for i in range(1, n_tp):
-        total = total + stats[i]
-    factor = lax.rsqrt(total / (width * n_tp) + EPSILON)
-    scale[...] = jnp.broadcast_to(factor[0:1, :], (128, rows)).T
+        share(shift).start()
 
     def to_peers(index, dst, send_sem, recv_sem):
         own = pl.ds(pl.multiple_of(e * cap, cap), cap)
@@ -185,9 +174,7 @@
         )
 
     def dispatch(s, m, index, dst):
-        gain = gains[s, :, pl.ds(pl.multiple_of(m * wide, wide), wide)]
-        normed = tok[s, m].astype(F32) * scale[:, 0:1] * gain
-        placed = jnp.dot(dmat[...], normed.astype(BF16), preferred_element_type=F32)
+        placed = jnp.dot(dmat[...], tok[s, m], preferred_element_type=F32)
         send[index] = placed.astype(BF16)
         to_peers(index, dst, xs.at[index], xr.at[index])
 
@@ -219,6 +206,39 @@
             along(1, z, n_tok + a, slot_in.at[z, a]).start()
 
         gate_up(slot_in.at[z, a], column(z, n_tok + a), first=a == 0)
+
+    def scale_to(p):
+        return remote("ep", p, rowscale.at[e], rowscale.at[e], sc_send.at[0], sc_recv.at[0])
+
+    def all_scales():
+        most = pl.ds(0, n_ep - 1)
+        return remote(
+            "ep", lax.rem(e + 1, n_ep), rowscale.at[most], rowscale.at[most], sc_send.at[0], sc_recv.at[0]
+        )
+
+    def send_scales():
+        for shift in range(1, n_tp):
+            share(shift).wait_recv()
+        total = stats[0]
+        for i in range(1, n_tp):
+            total = total + stats[i]
+        factor = lax.rsqrt(total / (width * n_tp) + EPSILON)
+        by_slot = lax.dot_general(
+            factor,
+            dmat[...].astype(F32),
+            (((1,), (1,)), ((), ())),
+            precision=lax.Precision.HIGHEST,
+            preferred_element_type=F32,
+        )
+        rowscale[e] = by_slot[0:1, :]
+        each_peer(lambda p: scale_to(p).start())
+
+    def turn_scales():
+        all_scales().wait_recv()
+        for block in range(n_ep):
+            turned[...] = jnp.broadcast_to(rowscale[block], (8, slots)).T
+            own = turned[pl.ds(pl.multiple_of(e * cap, cap), cap), 0:1]
+            slotscale[block * cap : (block + 1) * cap, :] = jnp.broadcast_to(own, (cap, 128))
 
     def arrive(k, m, ref_of):
         @pl.when(z + k <= last)
@@ -252,6 +272,12 @@
             def _():
                 arrive(k, n_tok + a, lambda s: slot_in.at[s, a])
 
+        @pl.when(i == 2 * n_tok - 1)
+        def _():
+            send_scales()
+
+    turn_scales()
+
     for a in range(n_slot):
         @pl.loop(1, last)
         def _(k):
@@ -267,8 +293,9 @@
         s = nth(last)
         gate_up(slot_in.at[s, a], column(s, n_tok + a))
 
-    gate_act = acc[0]
-    hid[...] = (gate_act / (1.0 + jnp.exp(-gate_act)) * acc[1]).astype(BF16)
+    gate_act = acc[0] * slotscale[:, 0:1]
+    up_act = acc[1] * slotscale[:, 0:1]
+    hid[...] = (gate_act / (1.0 + jnp.exp(-gate_act)) * up_act).astype(BF16)
     weights[2].wait()
 
     def down(index, s, m):
@@ -284,6 +311,15 @@
 
     def far(k):
         return nth(last - k)
+
+    def down_tok(i):
+        all_peers(i, recv.at[i], xs.at[i], xr.at[i]).wait_send()
+        down(i, far(i // n_tok), i % n_tok)
+        to_peers(i, ret.at[i], ys.at[i], yr.at[i])
+
+    @pl.loop(0, n_tok)
+    def _(i):
+        down_tok(i)
 
     for a in range(n_slot):
         @pl.loop(0, n_tp)
@@ -299,12 +335,9 @@
             def _():
                 onward(1, k, s, n_tok + a, send.at[index], in_slot.at[a]).start()
 
-    @pl.loop(0, steps)
+    @pl.loop(n_tok, steps)
     def _(i):
-        k, j = i // n_tok, i % n_tok
-        all_peers(i, recv.at[i], xs.at[i], xr.at[i]).wait_send()
-        down(i, far(k), j)
-        to_peers(i, ret.at[i], ys.at[i], yr.at[i])
+        down_tok(i)
 
     for a in range(n_slot):
         @pl.loop(0, last)
@@ -406,9 +439,9 @@
             wmat[...], ret_slot[a], preferred_element_type=F32
         ).astype(BF16)
 
+    all_scales().wait_send()
     for shift in range(1, n_tp):
-        for copy in share(shift):
-            copy.wait_send()
+        share(shift).wait_send()
 
     @pl.loop(0, n_tp)
     def _(s):
@@ -468,9 +501,10 @@
         out_specs=vmem,
         scratch_shapes=[
             pltpu.VMEM((n_tp, items, rows, wide), BF16),
-            pltpu.VMEM((n_tp, 1, width), F32),
             pltpu.VMEM((n_tp, 8, rows), F32),
-            pltpu.VMEM((rows, 128), F32),
+            pltpu.VMEM((n_ep, 1, slots), F32),
+            pltpu.VMEM((slots, 8), F32),
+            pltpu.VMEM((slots, 128), F32),
             pltpu.VMEM((slots, rows), BF16),
             pltpu.VMEM((rows, slots), BF16),
             pltpu.VMEM((n_tp * items, slots, wide), BF16),
@@ -487,8 +521,10 @@
             pltpu.VMEM((n_slot, 2, n_tp, slots, wide), BF16),
             pltpu.VMEM((rows, wide), F32),
             dma((items + 3,)),
-            dma((n_tp, 2)),
-            dma((n_tp, 2)),
+            dma((n_tp,)),
+            dma((n_tp,)),
+            dma((1,)),
+            dma((1,)),
             dma((2, n_tp, items)),
             dma((n_tp, items)),
             dma((steps + n_slot,)),
@@ -503,9 +539,9 @@
         ),
     )(
         tokens,
-        norm_gain.astype(F32).reshape(1, width),
-        expert_ids,
-        gate_prob,
+        norm_gain,
+        expert_ids.T,
+        gate_prob.T,
         w_gate[0],
         w_up[0],
         w_down[0],

time: 168 us -> 159 us (0.946)
  Pallas kernels: 161 us -> 156 us
  local copies, waits for them, and re-layouts: 6.34 us -> 2.16 us
    pallas_call x1, Pallas kernels: 161 us -> 156 us  [local(): pl.pallas_call(kernel, out_shape=jax.ShapeDtypeStruct((rows, width), BF16...]
    unnamed x3 -> x1, local copies, waits for them, and re-layouts: 5.06 us -> 2.16 us
where the time goes in v1:
time: 159 us; the launch traced here: 158 us
  Pallas kernels  156 us (98%)
  local copies, waits for them, and re-layouts  2.16 us (1%)
    pallas_call x1, Pallas kernels, local(): pl.pallas_call(kernel, out_shape=jax.ShapeDtypeStruct((rows, width), BF16...  156 us

profile of v1, /device:TPU:1, one launch (start us, length us, event | category | flops | bytes accessed | tf_op | source)
XLA Modules:
  0.0 158.4 jit_solution(17998912032195756987)
XLA Ops:
  0.0 156.2 %shard_map.73 = bf16[256,1792]{1,0:T(8,128)(2,1)} custom-call(bf16[256,1792]{1,0:T(8,128)(2,1)} %tok_hbm.1, bf16[1792]{0:T(1024)(128)(2,1)} %gain_ref.1, s32[8,256]{1,0:T(8,128)} %bitcast.8, bf16[8,256]{1,0:T(8,128)(2,1)} %bitcast.9, bf16[7168,512]{1,0:T(8,128)(2,1)} %bitcast.5, bf16[7168,512]{1,0:T(8,128)(2,1)} %bitcast.6, bf16[512,7168]{1,0:T(8,128)(2,1)} %bitcast.7), custom_call_target="tpu_custom_call" | custom-call | tf_op jit(solution)/shard_map/pallas_call | solution.py:497
  156.2 2.2 %copy.9 = bf16[256,1792]{1,0:T(8,128)(2,1)} copy(bf16[256,1792]{1,0:T(8,128)(2,1)} %shard_map.73) | data formatting | bytes 1835008

commit v2 on v1

v2 whole, which is shorter than its diff:
```python
import functools

import jax
import jax.numpy as jnp
from jax import lax
from jax.experimental import pallas as pl
from jax.experimental.pallas import tpu as pltpu
from jax.sharding import PartitionSpec as P

TOP = 8
EXP_DEV = 8
SHARES = ((1, 3), (3, 1))
PARTS = 7
UNROLL = 8
EPSILON = 1e-06
BF16 = jnp.bfloat16
F32 = jnp.float32


def look_up(table, index):
    span = len(table) ** 2
    total = 0
    for i, value in enumerate(table):
        if value:
            total = total + value * (1 - ((index - i) * (index - i) + span - 1) // span)
    return total


def near_first(n_tp):
    table = []
    for z in range(n_tp):
        inner = 1 if z < n_tp / 2 else -1
        table += sorted(range(n_tp), key=lambda s: (abs(s - z), -inner * (s - z)))
    return table


class Half:
    def __init__(self, core, items):
        forth, back = (max(1, items * share // PARTS) for share in SHARES[core])
        self.core = core
        self.d_slot, self.d_tok = forth, items - forth
        self.r_slot, self.r_tok = back, items - back


def buffers(n_ep, n_tp, rows, width, cap, wide, units, halves):
    items = width // wide
    slots, some = n_ep * cap, n_ep // 2 * cap
    most_d = max(n_tp * half.d_tok + half.d_slot for half in halves)
    most_r = max(n_tp * half.r_tok + half.r_slot for half in halves)
    most_tok = max(half.r_tok for half in halves)
    dma = pltpu.SemaphoreType.DMA
    names = dict(
        tok=pltpu.VMEM((n_tp, items, rows, wide), BF16),
        stats=pltpu.VMEM((n_tp, 8, rows), F32),
        rowscale=pltpu.VMEM((n_ep, 1, slots), F32),
        turned=pltpu.VMEM((slots, 8), F32),
        slotscale=pltpu.VMEM((2, some, 128), F32),
        dmat=pltpu.VMEM((slots, rows), BF16),
        wmat=pltpu.VMEM((rows, slots), BF16),
        send=pltpu.VMEM((most_d, slots, wide), BF16),
        w_gate=pltpu.VMEM((n_tp * width, units), BF16),
        w_up=pltpu.VMEM((n_tp * width, units), BF16),
        w_down=pltpu.VMEM((units, n_tp * width), BF16),
        ret=pltpu.VMEM((most_r, slots, wide), BF16),
        in_tok=pltpu.VMEM((most_tok, n_tp + 1, rows, wide), BF16),
        part=pltpu.VMEM((rows, wide), F32),
        load_sem=dma((items + 3,)),
        st_send=dma((n_tp,)),
        st_recv=dma((n_tp,)),
        sc_send=dma((1,)),
        sc_recv=dma((1,)),
        zt_send=dma((2, n_tp, items)),
        zt_recv=dma((n_tp, items)),
        xs=dma((most_d,)),
        yr=dma((most_r,)),
        pt_send=dma((n_tp, items)),
        pt_recv=dma((2, n_tp, items)),
    )
    for half in halves:
        h = half.core
        names.update({
            f"recv{h}": pltpu.VMEM((n_tp * half.d_tok, some, wide), BF16),
            f"slot_in{h}": pltpu.VMEM((n_tp, half.d_slot, some, wide), BF16),
            f"acc{h}": pltpu.VMEM((2, some, units), F32),
            f"hid{h}": pltpu.VMEM((some, units), BF16),
            f"ysend{h}": pltpu.VMEM((n_tp * items, some, wide), BF16),
            f"in_slot{h}": pltpu.VMEM((half.r_slot, n_tp + 1, some, wide), BF16),
            f"zs_send{h}": dma((2, n_tp, half.d_slot)),
            f"zs_recv{h}": dma((n_tp, half.d_slot)),
            f"xr{h}": dma((n_tp * half.d_tok + half.d_slot,)),
            f"ys{h}": dma((n_tp * half.r_tok + half.r_slot,)),
            f"ps_send{h}": dma((n_tp, half.r_slot)),
            f"ps_recv{h}": dma((2, n_tp, half.r_slot)),
        })
    return names


def body(names, halves, n_ep, n_tp, rows, width, cap, wide, *refs):
    tok_hbm, gain_ref, ids_ref, prob_ref, gate_hbm, up_hbm, down_hbm, out_ref = refs[:8]
    r = dict(zip(names, refs[8:]))
    tok, send, ret, in_tok, part = (r[n] for n in ("tok", "send", "ret", "in_tok", "part"))
    w_gate, w_up, w_down = r["w_gate"], r["w_up"], r["w_down"]
    dmat, wmat, stats, rowscale = r["dmat"], r["wmat"], r["stats"], r["rowscale"]
    e, z = lax.axis_index("ep"), lax.axis_index("tp")
    core, seat = lax.rem(e, 2), e // 2
    last = n_tp - 1
    items = width // wide
    slots, n_src = n_ep * cap, n_ep // 2
    table = near_first(n_tp)

    def nth(k):
        return look_up(table, z * n_tp + k)

    def far(k):
        return nth(last - k)

    def column(s, m):
        return pl.multiple_of(s * width + m * wide, wide)

    def block(i):
        return pl.ds(pl.multiple_of(i * cap, cap), cap)

    def mine(half):
        return core == half.core

    def remote(axis, index, src, dst, send_sem, recv_sem):
        return pltpu.make_async_remote_copy(
            src_ref=src,
            dst_ref=dst,
            send_sem=send_sem,
            recv_sem=recv_sem,
            device_id={axis: index},
            device_id_type=pl.DeviceIdType.MESH,
        )

    def awaited(ref, count, send_sem, recv_sem):
        some = ref.at[pl.ds(0, count)]
        return remote("ep", lax.rem(e + 1, n_ep), some, some, send_sem, recv_sem)

    def repeat(first, past, fn):
        if past <= UNROLL:
            for i in range(first, past):
                fn(i)
        else:
            pl.loop(first, past)(fn)

    def each_peer(fn):
        repeat(1, n_ep, lambda shift: fn(lax.rem(e + shift, n_ep)))

    def next_to(way):
        return lax.rem(z + n_tp - 1 if way == 0 else z + 1, n_tp)

    loads = [
        pltpu.make_async_copy(
            tok_hbm.at[:, pl.ds(m * wide, wide)], tok.at[z, m], r["load_sem"].at[m]
        )
        for m in range(items)
    ]
    weights = [
        pltpu.make_async_copy(src, dst, r["load_sem"].at[items + i])
        for i, (src, dst) in enumerate(
            ((gate_hbm, w_gate), (up_hbm, w_up), (down_hbm, w_down))
        )
    ]
    for copy in loads + weights:
        copy.start()

    barrier = pltpu.get_barrier_semaphore()

    def greet(axis, index):
        pl.semaphore_signal(
            barrier, inc=1, device_id={axis: index}, device_id_type=pl.DeviceIdType.MESH
        )

    each_peer(lambda p: greet("ep", p))
    for shift in range(1, n_tp):
        greet("tp", lax.rem(z + shift, n_tp))

    ids = ids_ref[...].T
    prob = prob_ref[...].astype(F32).T
    lane = lax.broadcasted_iota(jnp.int32, (rows, 128), 1)
    picked = jnp.zeros((rows, 128), F32)
    chance = jnp.zeros((rows, 128), F32)
    for k in range(TOP):
        same = ids[:, k : k + 1] == lane
        picked = jnp.where(same, 1.0, picked)
        chance = jnp.where(same, prob[:, k : k + 1], chance)
    picked = picked.astype(BF16)
    earlier = (
        lax.broadcasted_iota(jnp.int32, (rows, rows), 1)
        < lax.broadcasted_iota(jnp.int32, (rows, rows), 0)
    )
    earlier = jnp.where(earlier, 1.0, 0.0).astype(BF16)
    before = jnp.dot(earlier, picked, preferred_element_type=F32).astype(BF16)
    spread_row = lax.broadcasted_iota(jnp.int32, (128, slots), 0)
    spread_col = lax.broadcasted_iota(jnp.int32, (128, slots), 1)
    spread = jnp.where(
        (spread_col >= spread_row * cap) & (spread_col < (spread_row + 1) * cap), 1.0, 0.0
    ).astype(BF16)
    is_picked = jnp.dot(picked, spread, preferred_element_type=F32)
    place = jnp.dot(before, spread, preferred_element_type=F32)
    weight = jnp.dot(chance.astype(BF16), spread, preferred_element_type=F32)
    position = lax.rem(lax.broadcasted_iota(jnp.int32, (rows, slots), 1), cap).astype(F32)
    hit = (is_picked > 0.5) & (place == position)
    wmat[...] = jnp.where(hit, weight, 0.0).astype(BF16)
    dmat[...] = jnp.where(hit, 1.0, 0.0).T.astype(BF16)

    pl.semaphore_wait(barrier, n_ep - 1 + n_tp - 1)

    def along(way, s, m):
        return remote(
            "tp", next_to(way), tok.at[s, m], tok.at[s, m],
            r["zt_send"].at[way, s, m], r["zt_recv"].at[s, m],
        )

    def along_slot(half, way, s, a):
        h = half.core
        ref = r[f"slot_in{h}"].at[s, a]
        return remote(
            "tp", next_to(way), ref, ref,
            r[f"zs_send{h}"].at[way, s, a], r[f"zs_recv{h}"].at[s, a],
        )

    def both_ways(copy):
        @pl.when(z > 0)
        def _():
            copy(0).start()

        @pl.when(z < last)
        def _():
            copy(1).start()

    square = jnp.zeros((rows, wide), F32)
    gain = gain_ref[...].astype(F32).reshape(1, width)
    for m in range(items):
        loads[m].wait()
        values = tok[z, m].astype(F32)
        square = square + values * values
        tok[z, m] = (values * gain[:, m * wide : (m + 1) * wide]).astype(BF16)
        if m < halves[0].d_tok:
            @pl.when(mine(halves[0]))
            def _():
                both_ways(lambda way: along(way, z, m))

    square = jnp.sum(square, axis=1, keepdims=True)
    stats[z] = jnp.broadcast_to(square, (rows, 128)).T[0:8, :]

    def share(shift):
        ref = stats.at[z]
        peer = lax.rem(z + shift, n_tp)
        return remote("tp", peer, ref, ref, r["st_send"].at[shift], r["st_recv"].at[shift])

    for shift in range(1, n_tp):
        share(shift).start()

    def dispatch(half, s, m, index, dst):
        placed = jnp.dot(dmat[...], tok[s, m], preferred_element_type=F32)
        send[index] = placed.astype(BF16)
        dst[block(seat), :] = send[index, block(e), :]
        sems = r["xs"].at[index], r[f"xr{half.core}"].at[index]
        each_peer(
            lambda p: remote("ep", p, send.at[index, block(p)], dst.at[block(seat)], *sems).start()
        )

    def wait_in(half, index, dst):
        sems = r["xs"].at[index], r[f"xr{half.core}"].at[index]

        @pl.when(mine(half))
        def _():
            awaited(dst, (n_src - 1) * cap, *sems).wait_recv()

        @pl.when(core != half.core)
        def _():
            awaited(dst, n_src * cap, *sems).wait_recv()

    def wait_out(half):
        @pl.when(mine(half))
        def _():
            @pl.loop(0, n_tp * half.d_tok + half.d_slot)
            def _(i):
                sem = r["xs"].at[i]
                awaited(send.at[i], (n_ep - 1) * cap, sem, sem).wait_send()

    def gate_up(half, chunk, row, first=False):
        acc = r[f"acc{half.core}"]
        values = chunk[...]
        at = pl.ds(row, wide)
        for i, matrix in enumerate((w_gate, w_up)):
            product = jnp.dot(values, matrix[at, :], preferred_element_type=F32)
            acc[i] = product if first else acc[i] + product

    def slot_ref(half):
        slot_in = r[f"slot_in{half.core}"]
        return lambda s, a: slot_in.at[s, a]

    def own_slots_out(half):
        @pl.when(mine(half))
        def _():
            for a in range(half.d_slot):
                index = n_tp * half.d_tok + a
                dispatch(half, z, half.d_tok + a, index, slot_ref(half)(z, a))

    def own_toks_out(half):
        @pl.when(mine(half))
        def _():
            @pl.loop(0, half.d_tok)
            def _(j):
                dispatch(half, z, j, j, r[f"recv{half.core}"].at[j])

    def own_slots_in(half):
        for a in range(half.d_slot):
            ref = slot_ref(half)(z, a)
            wait_in(half, n_tp * half.d_tok + a, ref)
            both_ways(lambda way: along_slot(half, way, z, a))

    def own_slots_used(half):
        for a in range(half.d_slot):
            gate_up(half, slot_ref(half)(z, a), column(z, half.d_tok + a), first=a == 0)

    def arrive(k, copy):
        @pl.when(z + k <= last)
        def _():
            copy(0, z + k).wait_recv()

            @pl.when(z > 0)
            def _():
                copy(0, z + k).start()

        @pl.when(z - k >= 0)
        def _():
            copy(1, z - k).wait_recv()

            @pl.when(z < last)
            def _():
                copy(1, z - k).start()

    def tok_on(half, k, j):
        @pl.when(mine(half))
        def _():
            arrive(k, lambda way, s: along(way, s, j))
            index = k * half.d_tok + j
            dispatch(half, nth(k), j, index, r[f"recv{half.core}"].at[index])

    def slots_on(half, k):
        for a in range(half.d_slot):
            arrive(k, lambda way, s: along_slot(half, way, s, a))

    def slots_used(half, k):
        s = nth(k)
        for a in range(half.d_slot):
            gate_up(half, slot_ref(half)(s, a), column(s, half.d_tok + a))

    def take_in(half, k, j):
        index = k * half.d_tok + j
        ref = r[f"recv{half.core}"].at[index]
        wait_in(half, index, ref)
        gate_up(half, ref, column(nth(k), j))

    def take_in_all(half, first, past):
        @pl.loop(first * half.d_tok, past * half.d_tok)
        def _(i):
            take_in(half, i // half.d_tok, lax.rem(i, half.d_tok))

    def hidden(half):
        h = half.core
        scale = r["slotscale"][h, :, 0:1]
        gate_act = r[f"acc{h}"][0] * scale
        up_act = r[f"acc{h}"][1] * scale
        r[f"hid{h}"][...] = (gate_act / (1.0 + jnp.exp(-gate_act)) * up_act).astype(BF16)

    def scale_to(p):
        ref = rowscale.at[e]
        return remote("ep", p, ref, ref, r["sc_send"].at[0], r["sc_recv"].at[0])

    def all_scales():
        return awaited(rowscale, n_ep - 1, r["sc_send"].at[0], r["sc_recv"].at[0])

    def send_scales():
        for shift in range(1, n_tp):
            share(shift).wait_recv()
        total = stats[0]
        for i in range(1, n_tp):
            total = total + stats[i]
        factor = lax.rsqrt(total / (width * n_tp) + EPSILON)
        by_slot = lax.dot_general(
            factor,
            dmat[...].astype(F32),
            (((1,), (1,)), ((), ())),
            precision=lax.Precision.HIGHEST,
            preferred_element_type=F32,
        )
        rowscale[e] = by_slot[0:1, :]
        each_peer(lambda p: scale_to(p).start())

    def turn_scales():
        all_scales().wait_recv()
        for source in range(n_ep):
            r["turned"][...] = jnp.broadcast_to(rowscale[source], (8, slots)).T
            own = r["turned"][block(e), 0:1]
            at = source // 2 * cap
            r["slotscale"][source % 2, at : at + cap, :] = jnp.broadcast_to(own, (cap, 128))

    def down(half, index, s, m):
        matrix = w_down[:, pl.ds(column(s, m), wide)]
        h = half.core
        r[f"ysend{h}"][index] = jnp.dot(
            r[f"hid{h}"][...], matrix, preferred_element_type=F32
        ).astype(BF16)

    def to_owners(half, index, slot):
        ysend = r[f"ysend{half.core}"]
        sems = r[f"ys{half.core}"].at[slot], r["yr"].at[slot]

        def to_seat(shift):
            q = lax.rem(seat + shift, n_src)
            remote(
                "ep", 2 * q + half.core, ysend.at[index, block(q)], ret.at[slot, block(e)], *sems
            ).start()

        @pl.when(mine(half))
        def _():
            ret[slot, block(e), :] = ysend[index, block(seat), :]

        @pl.when(core != half.core)
        def _():
            to_seat(0)

        repeat(1, n_src, to_seat)

    def sent_to_owners(half, slot):
        sem = r[f"ys{half.core}"].at[slot]
        ref = r[f"ysend{half.core}"].at[0]

        @pl.when(mine(half))
        def _():
            awaited(ref, (n_src - 1) * cap, sem, sem).wait_send()

        @pl.when(core != half.core)
        def _():
            awaited(ref, n_src * cap, sem, sem).wait_send()

    def seat_of(way, s):
        if way == 0:
            return s
        return s + (n_tp - s) * (1 - (z - 1 - s + n_tp - 1) // n_tp)

    def onward(way, k, s, m, src):
        return remote(
            "tp", next_to(1 - way), src, in_tok.at[m, seat_of(way, s)],
            r["pt_send"].at[k, m], r["pt_recv"].at[way, s, m],
        )

    def onward_slot(half, way, k, s, a, src):
        h = half.core
        return remote(
            "tp", next_to(1 - way), src, r[f"in_slot{h}"].at[a, seat_of(way, s)],
            r[f"ps_send{h}"].at[k, a], r[f"ps_recv{h}"].at[way, s, a],
        )

    def slot_index(half, k, a):
        return n_tp * half.r_tok + k * half.r_slot + a

    def toks_down(half, first, past):
        @pl.loop(first * half.r_tok, past * half.r_tok)
        def _(i):
            down(half, i, far(i // half.r_tok), lax.rem(i, half.r_tok))
            to_owners(half, i, i)

    def slots_down(half, first, past):
        @pl.loop(first, past)
        def _(k):
            for a in range(half.r_slot):
                s, index = far(k), slot_index(half, k, a)
                down(half, index, s, half.r_tok + a)
                ref = r[f"ysend{half.core}"].at[index]

                @pl.when((z == 0) & (k < last))
                def _():
                    onward_slot(half, 0, k, s, a, ref).start()

                @pl.when((z == last) & (k < last))
                def _():
                    onward_slot(half, 1, k, s, a, ref).start()

    def slots_pass(half, k):
        ysend, in_slot = r[f"ysend{half.core}"], r[f"in_slot{half.core}"]
        s = far(k)
        for a in range(half.r_slot):
            index = slot_index(half, k, a)

            def pass_on(way):
                copy = onward_slot(half, way, k, s, a, ysend.at[index])
                awaited_here = remote(
                    "tp", next_to(way), in_slot.at[a, s], in_slot.at[a, s],
                    r[f"ps_send{half.core}"].at[k, a], r[f"ps_recv{half.core}"].at[way, s, a],
                )
                awaited_here.wait_recv()
                summed = ysend[index].astype(F32) + in_slot[a, s].astype(F32)
                ysend[index] = summed.astype(BF16)
                copy.start()

            @pl.when((s > z) & (z > 0))
            def _():
                pass_on(0)

            @pl.when((s < z) & (z < last))
            def _():
                pass_on(1)

    def own_slots_back(half):
        ysend, in_slot = r[f"ysend{half.core}"], r[f"in_slot{half.core}"]
        for a in range(half.r_slot):
            index = slot_index(half, last, a)

            def add(way, at):
                ref = in_slot.at[a, at]
                remote(
                    "tp", next_to(way), ref, ref,
                    r[f"ps_send{half.core}"].at[0, a], r[f"ps_recv{half.core}"].at[way, z, a],
                ).wait_recv()
                summed = ysend[index].astype(F32) + in_slot[a, at].astype(F32)
                ysend[index] = summed.astype(BF16)

            @pl.when(z > 0)
            def _():
                add(0, z)

            @pl.when(z < last)
            def _():
                add(1, n_tp)

            to_owners(half, index, n_tp * half.r_tok + a)

    def combine(i):
        sem = r["yr"].at[i]
        awaited(ret.at[i], (n_ep - 1) * cap, sem, sem).wait_recv()
        return jnp.dot(wmat[...], ret[i], preferred_element_type=F32)

    def add_in(way, s, at, j):
        ref = in_tok.at[j, at]
        remote(
            "tp", next_to(way), ref, ref, r["pt_send"].at[0, j], r["pt_recv"].at[way, s, j]
        ).wait_recv()
        part[...] = part[...] + in_tok[j, at].astype(F32)

    def parts_on(half, first, past, where=True):
        @pl.when(mine(half) & where)
        def _():
            @pl.loop(first * half.r_tok, past * half.r_tok)
            def _(i):
                k, j = i // half.r_tok, lax.rem(i, half.r_tok)
                s = far(k)
                part[...] = combine(i)

                @pl.when((s > z) & (z > 0))
                def _():
                    add_in(0, s, s, j)

                @pl.when((s < z) & (z < last))
                def _():
                    add_in(1, s, s, j)

                send[i, 0:rows, :] = part[...].astype(BF16)
                ref = send.at[i, pl.ds(0, rows)]

                @pl.when(s > z)
                def _():
                    onward(0, k, s, j, ref).start()

                @pl.when(s < z)
                def _():
                    onward(1, k, s, j, ref).start()

    def finish(half):
        @pl.when(mine(half))
        def _():
            @pl.loop(0, half.r_tok)
            def _(j):
                part[...] = combine(last * half.r_tok + j)

                @pl.when(z > 0)
                def _():
                    add_in(0, z, z, j)

                @pl.when(z < last)
                def _():
                    add_in(1, z, n_tp, j)

                out_ref[:, pl.ds(pl.multiple_of(j * wide, wide), wide)] = part[...].astype(BF16)

            for a in range(half.r_slot):
                m = half.r_tok + a
                out_ref[:, m * wide : (m + 1) * wide] = combine(n_tp * half.r_tok + a).astype(BF16)

    one, two = halves
    at_end = (z == 0) | (z == last)
    inside = (z > 0) & (z < last)

    own_slots_out(one)
    own_toks_out(one)
    weights[0].wait()
    weights[1].wait()
    own_slots_in(one)
    own_slots_used(one)

    @pl.loop(one.d_tok, n_tp * one.d_tok)
    def _(i):
        k, j = i // one.d_tok, lax.rem(i, one.d_tok)
        tok_on(one, k, j)
        take_in(one, k - 1, j)

        @pl.when((j == one.d_tok - 1) & (k < last))
        def _():
            slots_on(one, k)

        @pl.when(i == 2 * one.d_tok - 1)
        def _():
            send_scales()

    @pl.when(mine(two))
    def _():
        for m in range(two.d_tok):
            both_ways(lambda way: along(way, z, m))

    own_slots_out(two)
    turn_scales()

    @pl.loop(1, last)
    def _(k):
        slots_used(one, k)

    take_in_all(one, last, n_tp)
    own_toks_out(two)
    slots_on(one, last)
    slots_used(one, last)
    own_slots_in(two)
    hidden(one)
    weights[2].wait()
    wait_out(one)

    def toks_on(half, k):
        @pl.loop(0, half.d_tok)
        def _(j):
            tok_on(half, k, j)

    slots_down(one, 0, 1)
    toks_down(one, 0, 1)
    toks_on(two, 1)
    slots_down(one, 1, n_tp)
    toks_down(one, 1, n_tp)
    own_slots_used(two)
    slots_on(two, 1)
    for k in range(2, last):
        slots_pass(one, k - 2)
        toks_on(two, k)
        parts_on(one, k - 2, k - 1, at_end)
        slots_pass(one, k - 1)
        if k < last - 1:
            slots_on(two, k)
    slots_pass(one, last - 1)
    toks_on(two, last)
    parts_on(one, last - 2, last, at_end)
    slots_on(two, last - 1)
    own_slots_back(one)
    parts_on(one, 0, 1, inside)
    take_in_all(two, 0, 1)
    parts_on(one, 1, last - 1, inside)
    take_in_all(two, 1, last)
    parts_on(one, last - 1, last, inside)

    @pl.loop(1, last)
    def _(k):
        slots_used(two, k)

    take_in_all(two, last, n_tp)
    slots_on(two, last)
    slots_used(two, last)
    hidden(two)
    wait_out(two)

    toks_down(two, 0, 1)
    slots_down(two, 0, n_tp)
    toks_down(two, 1, n_tp)
    finish(one)
    for k in range(last):
        slots_pass(two, k)
    parts_on(two, 0, 1)
    own_slots_back(two)
    parts_on(two, 1, last)
    finish(two)

    all_scales().wait_send()
    for shift in range(1, n_tp):
        share(shift).wait_send()

    for half in halves:
        @pl.loop(0, n_tp)
        def _(s):
            for way, sends in enumerate(((z > 0) & (s >= z), (z < last) & (s <= z))):
                @pl.when(sends)
                def _():
                    for a in range(half.d_slot):
                        along_slot(half, way, s, a).wait_send()

                    @pl.when(mine(half))
                    def _():
                        for m in range(half.d_tok):
                            along(way, s, m).wait_send()

        @pl.loop(0, n_tp * half.r_tok + half.r_slot)
        def _(i):
            sent_to_owners(half, i)

        @pl.loop(0, last)
        def _(k):
            for a in range(half.r_slot):
                onward_slot(half, 0, k, 0, a, r[f"ysend{half.core}"].at[0]).wait_send()

            @pl.when(mine(half))
            def _():
                for m in range(half.r_tok):
                    onward(0, k, 0, m, send.at[0, pl.ds(0, rows)]).wait_send()


def local(tokens, norm_gain, expert_ids, gate_prob, w_gate, w_up, w_down):
    n_ep = lax.axis_size("ep")
    n_tp = lax.axis_size("tp")
    rows, width = tokens.shape
    cap = max(2, 2 * rows * TOP // (EXP_DEV * n_ep))
    wide = 256 if width % 256 == 0 else 128
    halves = [Half(core, width // wide) for core in range(2)]
    names = buffers(n_ep, n_tp, rows, width, cap, wide, w_gate.shape[2], halves)
    kernel = functools.partial(
        body, list(names), halves, n_ep, n_tp, rows, width, cap, wide
    )
    vmem = pl.BlockSpec(memory_space=pltpu.VMEM)
    hbm = pl.BlockSpec(memory_space=pl.ANY)
    return pl.pallas_call(
        kernel,
        out_shape=jax.ShapeDtypeStruct((rows, width), BF16),
        in_specs=[hbm, vmem, vmem, vmem, hbm, hbm, hbm],
        out_specs=vmem,
        scratch_shapes=list(names.values()),
        compiler_params=pltpu.CompilerParams(
            collective_id=0, has_side_effects=True, vmem_limit_bytes=67043328
        ),
        name="moe",
    )(
        tokens,
        norm_gain,
        expert_ids.T,
        gate_prob.T,
        w_gate[0],
        w_up[0],
        w_down[0],
    )


def solution(mesh):
    placed = (
        P("ep", "tp"),
        P("tp"),
        P("ep", None),
        P("ep", None),
        P("ep", None, "tp"),
        P("ep", None, "tp"),
        P("ep", "tp", None),
    )
    return jax.shard_map(
        local, mesh=mesh, in_specs=placed, out_specs=P("ep", "tp"), check_vma=False
    )
```

time: 159 us -> 146 us (0.918)
  Pallas kernels: 156 us -> 144 us
    pallas_call x1, Pallas kernels: 156 us -> 144 us  [local(): pl.pallas_call(kernel, out_shape=jax.ShapeDtypeStruct((rows, width), BF16...]
where the time goes in v2:
time: 146 us
  Pallas kernels  144 us (99%)
  local copies, waits for them, and re-layouts  2.16 us (1%)
    pallas_call x1, Pallas kernels, local(): pl.pallas_call(kernel, out_shape=jax.ShapeDtypeStruct((rows, width), BF16...  144 us

profile of v2, /device:TPU:1, one launch (start us, length us, event | category | flops | bytes accessed | tf_op | source)
XLA Modules:
  0.0 145.9 jit_solution(8548805757005790713)
XLA Ops:
  0.0 143.7 %moe.1 = bf16[256,1792]{1,0:T(8,128)(2,1)} custom-call(bf16[256,1792]{1,0:T(8,128)(2,1)} %refs_0_.1, bf16[1792]{0:T(1024)(128)(2,1)} %refs_1_.1, s32[8,256]{1,0:T(8,128)} %bitcast.8, bf16[8,256]{1,0:T(8,128)(2,1)} %bitcast.9, bf16[7168,512]{1,0:T(8,128)(2,1)} %bitcast.5, bf16[7168,512]{1,0:T(8,128)(2,1)} %bitcast.6, bf16[512,7168]{1,0:T(8,128)(2,1)} %bitcast.7), custom_call_target="tpu_custom_call" | custom-call | tf_op jit(solution)/shard_map/moe/pallas_call | solution.py:738
  143.7 2.2 %copy.9 = bf16[256,1792]{1,0:T(8,128)(2,1)} copy(bf16[256,1792]{1,0:T(8,128)(2,1)} %moe.1) | data formatting | bytes 1835008

commit v3 on v2

--- a/solution.py
+++ b/solution.py
@@ -64,7 +64,9 @@
         ret=pltpu.VMEM((most_r, slots, wide), BF16),
         in_tok=pltpu.VMEM((most_tok, n_tp + 1, rows, wide), BF16),
         part=pltpu.VMEM((rows, wide), F32),
+        result=pltpu.VMEM((items, rows, wide), BF16),
         load_sem=dma((items + 3,)),
+        out_sem=dma((items,)),
         st_send=dma((n_tp,)),
         st_recv=dma((n_tp,)),
         sc_send=dma((1,)),
@@ -96,7 +98,7 @@
 
 
 def body(names, halves, n_ep, n_tp, rows, width, cap, wide, *refs):
-    tok_hbm, gain_ref, ids_ref, prob_ref, gate_hbm, up_hbm, down_hbm, out_ref = refs[:8]
+    tok_hbm, gain_ref, ids_ref, prob_ref, gate_hbm, up_hbm, down_hbm, out_hbm = refs[:8]
     r = dict(zip(names, refs[8:]))
     tok, send, ret, in_tok, part = (r[n] for n in ("tok", "send", "ret", "in_tok", "part"))
     w_gate, w_up, w_down = r["w_gate"], r["w_up"], r["w_down"]
@@ -571,6 +573,10 @@
                 def _():
                     onward(1, k, s, j, ref).start()
 
+    def write(m):
+        columns = pl.ds(pl.multiple_of(m * wide, wide), wide)
+        return pltpu.make_async_copy(r["result"].at[m], out_hbm.at[:, columns], r["out_sem"].at[m])
+
     def finish(half):
         @pl.when(mine(half))
         def _():
@@ -586,11 +592,23 @@
                 def _():
                     add_in(1, z, n_tp, j)
 
-                out_ref[:, pl.ds(pl.multiple_of(j * wide, wide), wide)] = part[...].astype(BF16)
+                r["result"][j] = part[...].astype(BF16)
+
+                @pl.when(j > 0)
+                def _():
+                    write(j - 1).start()
 
             for a in range(half.r_slot):
                 m = half.r_tok + a
-                out_ref[:, m * wide : (m + 1) * wide] = combine(n_tp * half.r_tok + a).astype(BF16)
+                r["result"][m] = combine(n_tp * half.r_tok + a).astype(BF16)
+                write(m - 1).start()
+
+            write(items - 1).start()
+
+    def toks_on(half, k):
+        @pl.loop(0, half.d_tok)
+        def _(j):
+            tok_on(half, k, j)
 
     one, two = halves
     at_end = (z == 0) | (z == last)
@@ -638,40 +656,32 @@
     weights[2].wait()
     wait_out(one)
 
-    def toks_on(half, k):
-        @pl.loop(0, half.d_tok)
-        def _(j):
-            tok_on(half, k, j)
-
     slots_down(one, 0, 1)
     toks_down(one, 0, 1)
     toks_on(two, 1)
     slots_down(one, 1, n_tp)
-    toks_down(one, 1, n_tp)
+    toks_down(one, 1, last)
     own_slots_used(two)
-    slots_on(two, 1)
-    for k in range(2, last):
+    take_in_all(two, 0, 1)
+    if last > 1:
+        slots_on(two, 1)
+        slots_used(two, 1)
+    for k in range(2, n_tp):
         slots_pass(one, k - 2)
         toks_on(two, k)
-        parts_on(one, k - 2, k - 1, at_end)
-        slots_pass(one, k - 1)
-        if k < last - 1:
-            slots_on(two, k)
+        if k < last:
+            parts_on(one, k - 2, k - 1, at_end)
     slots_pass(one, last - 1)
-    toks_on(two, last)
-    parts_on(one, last - 2, last, at_end)
-    slots_on(two, last - 1)
+    parts_on(one, max(0, last - 2), last, at_end)
+    for k in range(2, last):
+        slots_on(two, k)
+        slots_used(two, k)
+    take_in_all(two, 1, last - 1)
     own_slots_back(one)
+    toks_down(one, last, n_tp)
     parts_on(one, 0, 1, inside)
-    take_in_all(two, 0, 1)
+    take_in_all(two, last - 1, last)
     parts_on(one, 1, last - 1, inside)
-    take_in_all(two, 1, last)
-    parts_on(one, last - 1, last, inside)
-
-    @pl.loop(1, last)
-    def _(k):
-        slots_used(two, k)
-
     take_in_all(two, last, n_tp)
     slots_on(two, last)
     slots_used(two, last)
@@ -680,18 +690,36 @@
 
     toks_down(two, 0, 1)
     slots_down(two, 0, n_tp)
+    parts_on(one, last - 1, last, inside)
     toks_down(two, 1, n_tp)
     finish(one)
     for k in range(last):
         slots_pass(two, k)
     parts_on(two, 0, 1)
     own_slots_back(two)
-    parts_on(two, 1, last)
-    finish(two)
 
     all_scales().wait_send()
     for shift in range(1, n_tp):
         share(shift).wait_send()
+
+    def onward_done(half):
+        @pl.loop(0, last)
+        def _(k):
+            for a in range(half.r_slot):
+                onward_slot(half, 0, k, 0, a, r[f"ysend{half.core}"].at[0]).wait_send()
+
+    def parts_done(half, first, past):
+        @pl.when(mine(half))
+        def _():
+            @pl.loop(first, past)
+            def _(k):
+                for m in range(half.r_tok):
+                    onward(0, k, 0, m, send.at[0, pl.ds(0, rows)]).wait_send()
+
+    def owners_done(half, first, past):
+        @pl.loop(first, past)
+        def _(i):
+            sent_to_owners(half, i)
 
     for half in halves:
         @pl.loop(0, n_tp)
@@ -707,19 +735,18 @@
                         for m in range(half.d_tok):
                             along(way, s, m).wait_send()
 
-        @pl.loop(0, n_tp * half.r_tok + half.r_slot)
-        def _(i):
-            sent_to_owners(half, i)
-
-        @pl.loop(0, last)
-        def _(k):
-            for a in range(half.r_slot):
-                onward_slot(half, 0, k, 0, a, r[f"ysend{half.core}"].at[0]).wait_send()
-
-            @pl.when(mine(half))
-            def _():
-                for m in range(half.r_tok):
-                    onward(0, k, 0, m, send.at[0, pl.ds(0, rows)]).wait_send()
+    owners_done(one, 0, n_tp * one.r_tok + one.r_slot)
+    onward_done(one)
+    parts_done(one, 0, last)
+    parts_on(two, 1, last)
+    owners_done(two, 0, last * two.r_tok)
+    onward_done(two)
+    parts_done(two, 0, last - 1)
+    finish(two)
+    parts_done(two, last - 1, last)
+    owners_done(two, last * two.r_tok, n_tp * two.r_tok + two.r_slot)
+    for m in range(items):
+        write(m).wait()
 
 
 def local(tokens, norm_gain, expert_ids, gate_prob, w_gate, w_up, w_down):
@@ -739,7 +766,7 @@
         kernel,
         out_shape=jax.ShapeDtypeStruct((rows, width), BF16),
         in_specs=[hbm, vmem, vmem, vmem, hbm, hbm, hbm],
-        out_specs=vmem,
+        out_specs=hbm,
         scratch_shapes=list(names.values()),
         compiler_params=pltpu.CompilerParams(
             collective_id=0, has_side_effects=True, vmem_limit_bytes=67043328

time: 146 us -> 143 us (0.979)
  Pallas kernels: 144 us -> 141 us
    pallas_call x1, Pallas kernels: 144 us -> 141 us  [local(): pl.pallas_call(kernel, out_shape=jax.ShapeDtypeStruct((rows, width), BF16...]
where the time goes in v3:
time: 143 us
  Pallas kernels  141 us (99%)
  local copies, waits for them, and re-layouts  2.16 us (2%)
    pallas_call x1, Pallas kernels, local(): pl.pallas_call(kernel, out_shape=jax.ShapeDtypeStruct((rows, width), BF16...  141 us

profile of v3, /device:TPU:1, one launch (start us, length us, event | category | flops | bytes accessed | tf_op | source)
XLA Modules:
  0.0 142.9 jit_solution(2753561970286490746)
XLA Ops:
  0.0 140.7 %moe.1 = bf16[256,1792]{1,0:T(8,128)(2,1)} custom-call(bf16[256,1792]{1,0:T(8,128)(2,1)} %refs_0_.1, bf16[1792]{0:T(1024)(128)(2,1)} %refs_1_.1, s32[8,256]{1,0:T(8,128)} %bitcast.8, bf16[8,256]{1,0:T(8,128)(2,1)} %bitcast.9, bf16[7168,512]{1,0:T(8,128)(2,1)} %bitcast.5, bf16[7168,512]{1,0:T(8,128)(2,1)} %bitcast.6, bf16[512,7168]{1,0:T(8,128)(2,1)} %bitcast.7), custom_call_target="tpu_custom_call" | custom-call | tf_op jit(solution)/shard_map/moe/pallas_call | solution.py:765
  140.7 2.2 %copy.9 = bf16[256,1792]{1,0:T(8,128)(2,1)} copy(bf16[256,1792]{1,0:T(8,128)(2,1)} %moe.1) | data formatting | bytes 1835008

commit v4 on v3

--- a/solution.py
+++ b/solution.py
@@ -67,16 +67,16 @@
         result=pltpu.VMEM((items, rows, wide), BF16),
         load_sem=dma((items + 3,)),
         out_sem=dma((items,)),
-        st_send=dma((n_tp,)),
-        st_recv=dma((n_tp,)),
+        st_send=dma((1,)),
+        st_recv=dma((1,)),
         sc_send=dma((1,)),
         sc_recv=dma((1,)),
-        zt_send=dma((2, n_tp, items)),
+        zt_send=dma((2, n_tp)),
         zt_recv=dma((n_tp, items)),
-        xs=dma((most_d,)),
+        xs=dma((1,)),
         yr=dma((most_r,)),
-        pt_send=dma((n_tp, items)),
-        pt_recv=dma((2, n_tp, items)),
+        pt_send=dma((1,)),
+        pt_recv=dma((n_tp + 1, most_tok)),
     )
     for half in halves:
         h = half.core
@@ -87,12 +87,12 @@
             f"hid{h}": pltpu.VMEM((some, units), BF16),
             f"ysend{h}": pltpu.VMEM((n_tp * items, some, wide), BF16),
             f"in_slot{h}": pltpu.VMEM((half.r_slot, n_tp + 1, some, wide), BF16),
-            f"zs_send{h}": dma((2, n_tp, half.d_slot)),
+            f"zs_send{h}": dma((2, n_tp)),
             f"zs_recv{h}": dma((n_tp, half.d_slot)),
             f"xr{h}": dma((n_tp * half.d_tok + half.d_slot,)),
-            f"ys{h}": dma((n_tp * half.r_tok + half.r_slot,)),
-            f"ps_send{h}": dma((n_tp, half.r_slot)),
-            f"ps_recv{h}": dma((2, n_tp, half.r_slot)),
+            f"ys{h}": dma((1,)),
+            f"ps_send{h}": dma((1,)),
+            f"ps_recv{h}": dma((n_tp + 1, half.r_slot)),
         })
     return names
 
@@ -145,6 +145,10 @@
                 fn(i)
         else:
             pl.loop(first, past)(fn)
+
+    def sent(buffer, chunks, count, sem):
+        some = buffer.at[pl.ds(0, chunks), pl.ds(0, count)]
+        remote("ep", lax.rem(e + 1, n_ep), some, some, sem, sem).wait_send()
 
     def each_peer(fn):
         repeat(1, n_ep, lambda shift: fn(lax.rem(e + shift, n_ep)))
@@ -212,7 +216,7 @@
     def along(way, s, m):
         return remote(
             "tp", next_to(way), tok.at[s, m], tok.at[s, m],
-            r["zt_send"].at[way, s, m], r["zt_recv"].at[s, m],
+            r["zt_send"].at[way, s], r["zt_recv"].at[s, m],
         )
 
     def along_slot(half, way, s, a):
@@ -220,7 +224,7 @@
         ref = r[f"slot_in{h}"].at[s, a]
         return remote(
             "tp", next_to(way), ref, ref,
-            r[f"zs_send{h}"].at[way, s, a], r[f"zs_recv{h}"].at[s, a],
+            r[f"zs_send{h}"].at[way, s], r[f"zs_recv{h}"].at[s, a],
         )
 
     def both_ways(copy):
@@ -250,22 +254,25 @@
     def share(shift):
         ref = stats.at[z]
         peer = lax.rem(z + shift, n_tp)
-        return remote("tp", peer, ref, ref, r["st_send"].at[shift], r["st_recv"].at[shift])
+        return remote("tp", peer, ref, ref, r["st_send"].at[0], r["st_recv"].at[0])
 
     for shift in range(1, n_tp):
         share(shift).start()
+
+    def shares():
+        return awaited(stats, last, r["st_send"].at[0], r["st_recv"].at[0])
 
     def dispatch(half, s, m, index, dst):
         placed = jnp.dot(dmat[...], tok[s, m], preferred_element_type=F32)
         send[index] = placed.astype(BF16)
         dst[block(seat), :] = send[index, block(e), :]
-        sems = r["xs"].at[index], r[f"xr{half.core}"].at[index]
+        sems = r["xs"].at[0], r[f"xr{half.core}"].at[index]
         each_peer(
             lambda p: remote("ep", p, send.at[index, block(p)], dst.at[block(seat)], *sems).start()
         )
 
     def wait_in(half, index, dst):
-        sems = r["xs"].at[index], r[f"xr{half.core}"].at[index]
+        sems = r["xs"].at[0], r[f"xr{half.core}"].at[index]
 
         @pl.when(mine(half))
         def _():
@@ -278,10 +285,7 @@
     def wait_out(half):
         @pl.when(mine(half))
         def _():
-            @pl.loop(0, n_tp * half.d_tok + half.d_slot)
-            def _(i):
-                sem = r["xs"].at[i]
-                awaited(send.at[i], (n_ep - 1) * cap, sem, sem).wait_send()
+            sent(send, n_tp * half.d_tok + half.d_slot, (n_ep - 1) * cap, r["xs"].at[0])
 
     def gate_up(half, chunk, row, first=False):
         acc = r[f"acc{half.core}"]
@@ -378,8 +382,7 @@
         return awaited(rowscale, n_ep - 1, r["sc_send"].at[0], r["sc_recv"].at[0])
 
     def send_scales():
-        for shift in range(1, n_tp):
-            share(shift).wait_recv()
+        shares().wait_recv()
         total = stats[0]
         for i in range(1, n_tp):
             total = total + stats[i]
@@ -411,7 +414,7 @@
 
     def to_owners(half, index, slot):
         ysend = r[f"ysend{half.core}"]
-        sems = r[f"ys{half.core}"].at[slot], r["yr"].at[slot]
+        sems = r[f"ys{half.core}"].at[0], r["yr"].at[slot]
 
         def to_seat(shift):
             q = lax.rem(seat + shift, n_src)
@@ -429,34 +432,34 @@
 
         repeat(1, n_src, to_seat)
 
-    def sent_to_owners(half, slot):
-        sem = r[f"ys{half.core}"].at[slot]
-        ref = r[f"ysend{half.core}"].at[0]
-
-        @pl.when(mine(half))
-        def _():
-            awaited(ref, (n_src - 1) * cap, sem, sem).wait_send()
+    def owners_done(half):
+        sem = r[f"ys{half.core}"].at[0]
+        ysend, chunks = r[f"ysend{half.core}"], n_tp * half.r_tok + half.r_slot
+
+        @pl.when(mine(half))
+        def _():
+            sent(ysend, chunks, (n_src - 1) * cap, sem)
 
         @pl.when(core != half.core)
         def _():
-            awaited(ref, n_src * cap, sem, sem).wait_send()
+            sent(ysend, chunks, n_src * cap, sem)
 
     def seat_of(way, s):
         if way == 0:
             return s
         return s + (n_tp - s) * (1 - (z - 1 - s + n_tp - 1) // n_tp)
 
-    def onward(way, k, s, m, src):
+    def onward(way, s, m, src):
         return remote(
             "tp", next_to(1 - way), src, in_tok.at[m, seat_of(way, s)],
-            r["pt_send"].at[k, m], r["pt_recv"].at[way, s, m],
-        )
-
-    def onward_slot(half, way, k, s, a, src):
+            r["pt_send"].at[0], r["pt_recv"].at[seat_of(way, s), m],
+        )
+
+    def onward_slot(half, way, s, a, src):
         h = half.core
         return remote(
             "tp", next_to(1 - way), src, r[f"in_slot{h}"].at[a, seat_of(way, s)],
-            r[f"ps_send{h}"].at[k, a], r[f"ps_recv{h}"].at[way, s, a],
+            r[f"ps_send{h}"].at[0], r[f"ps_recv{h}"].at[seat_of(way, s), a],
         )
 
     def slot_index(half, k, a):
@@ -478,11 +481,11 @@
 
                 @pl.when((z == 0) & (k < last))
                 def _():
-                    onward_slot(half, 0, k, s, a, ref).start()
+                    onward_slot(half, 0, s, a, ref).start()
 
                 @pl.when((z == last) & (k < last))
                 def _():
-                    onward_slot(half, 1, k, s, a, ref).start()
+                    onward_slot(half, 1, s, a, ref).start()
 
     def slots_pass(half, k):
         ysend, in_slot = r[f"ysend{half.core}"], r[f"in_slot{half.core}"]
@@ -491,10 +494,10 @@
             index = slot_index(half, k, a)
 
             def pass_on(way):
-                copy = onward_slot(half, way, k, s, a, ysend.at[index])
+                copy = onward_slot(half, way, s, a, ysend.at[index])
                 awaited_here = remote(
                     "tp", next_to(way), in_slot.at[a, s], in_slot.at[a, s],
-                    r[f"ps_send{half.core}"].at[k, a], r[f"ps_recv{half.core}"].at[way, s, a],
+                    r[f"ps_send{half.core}"].at[0], r[f"ps_recv{half.core}"].at[s, a],
                 )
                 awaited_here.wait_recv()
                 summed = ysend[index].astype(F32) + in_slot[a, s].astype(F32)
@@ -518,7 +521,7 @@
                 ref = in_slot.at[a, at]
                 remote(
                     "tp", next_to(way), ref, ref,
-                    r[f"ps_send{half.core}"].at[0, a], r[f"ps_recv{half.core}"].at[way, z, a],
+                    r[f"ps_send{half.core}"].at[0], r[f"ps_recv{half.core}"].at[at, a],
                 ).wait_recv()
                 summed = ysend[index].astype(F32) + in_slot[a, at].astype(F32)
                 ysend[index] = summed.astype(BF16)
@@ -538,10 +541,10 @@
         awaited(ret.at[i], (n_ep - 1) * cap, sem, sem).wait_recv()
         return jnp.dot(wmat[...], ret[i], preferred_element_type=F32)
 
-    def add_in(way, s, at, j):
+    def add_in(way, at, j):
         ref = in_tok.at[j, at]
         remote(
-            "tp", next_to(way), ref, ref, r["pt_send"].at[0, j], r["pt_recv"].at[way, s, j]
+            "tp", next_to(way), ref, ref, r["pt_send"].at[0], r["pt_recv"].at[at, j]
         ).wait_recv()
         part[...] = part[...] + in_tok[j, at].astype(F32)
 
@@ -556,22 +559,22 @@
 
                 @pl.when((s > z) & (z > 0))
                 def _():
-                    add_in(0, s, s, j)
+                    add_in(0, s, j)
 
                 @pl.when((s < z) & (z < last))
                 def _():
-                    add_in(1, s, s, j)
+                    add_in(1, s, j)
 
                 send[i, 0:rows, :] = part[...].astype(BF16)
                 ref = send.at[i, pl.ds(0, rows)]
 
                 @pl.when(s > z)
                 def _():
-                    onward(0, k, s, j, ref).start()
+                    onward(0, s, j, ref).start()
 
                 @pl.when(s < z)
                 def _():
-                    onward(1, k, s, j, ref).start()
+                    onward(1, s, j, ref).start()
 
     def write(m):
         columns = pl.ds(pl.multiple_of(m * wide, wide), wide)
@@ -586,11 +589,11 @@
 
                 @pl.when(z > 0)
                 def _():
-                    add_in(0, z, z, j)
+                    add_in(0, z, j)
 
                 @pl.when(z < last)
                 def _():
-                    add_in(1, z, n_tp, j)
+                    add_in(1, n_tp, j)
 
                 r["result"][j] = part[...].astype(BF16)
 
@@ -699,27 +702,16 @@
     own_slots_back(two)
 
     all_scales().wait_send()
-    for shift in range(1, n_tp):
-        share(shift).wait_send()
+    shares().wait_send()
 
     def onward_done(half):
-        @pl.loop(0, last)
-        def _(k):
-            for a in range(half.r_slot):
-                onward_slot(half, 0, k, 0, a, r[f"ysend{half.core}"].at[0]).wait_send()
-
-    def parts_done(half, first, past):
-        @pl.when(mine(half))
-        def _():
-            @pl.loop(first, past)
-            def _(k):
-                for m in range(half.r_tok):
-                    onward(0, k, 0, m, send.at[0, pl.ds(0, rows)]).wait_send()
-
-    def owners_done(half, first, past):
-        @pl.loop(first, past)
-        def _(i):
-            sent_to_owners(half, i)
+        chunks = last * half.r_slot
+        sent(r[f"ysend{half.core}"], chunks, n_src * cap, r[f"ps_send{half.core}"].at[0])
+
+    def parts_done(half):
+        @pl.when(mine(half))
+        def _():
+            sent(send, last * half.r_tok, rows, r["pt_send"].at[0])
 
     for half in halves:
         @pl.loop(0, n_tp)
@@ -727,24 +719,26 @@
             for way, sends in enumerate(((z > 0) & (s >= z), (z < last) & (s <= z))):
                 @pl.when(sends)
                 def _():
-                    for a in range(half.d_slot):
-                        along_slot(half, way, s, a).wait_send()
+                    h = half.core
+                    awaited(
+                        r[f"slot_in{h}"].at[s], half.d_slot,
+                        r[f"zs_send{h}"].at[way, s], r[f"zs_recv{h}"].at[s, 0],
+                    ).wait_send()
 
                     @pl.when(mine(half))
                     def _():
-                        for m in range(half.d_tok):
-                            along(way, s, m).wait_send()
-
-    owners_done(one, 0, n_tp * one.r_tok + one.r_slot)
+                        awaited(
+                            tok.at[s], half.d_tok, r["zt_send"].at[way, s], r["zt_recv"].at[s, 0]
+                        ).wait_send()
+
+    owners_done(one)
     onward_done(one)
-    parts_done(one, 0, last)
+    parts_done(one)
     parts_on(two, 1, last)
-    owners_done(two, 0, last * two.r_tok)
     onward_done(two)
-    parts_done(two, 0, last - 1)
     finish(two)
-    parts_done(two, last - 1, last)
-    owners_done(two, last * two.r_tok, n_tp * two.r_tok + two.r_slot)
+    parts_done(two)
+    owners_done(two)
     for m in range(items):
         write(m).wait()
 

time: 143 us -> 141 us (0.986)
  Pallas kernels: 141 us -> 139 us
    pallas_call x1, Pallas kernels: 141 us -> 139 us  [local(): pl.pallas_call(kernel, out_shape=jax.ShapeDtypeStruct((rows, width), BF16...]
where the time goes in v4:
time: 141 us
  Pallas kernels  139 us (99%)
  local copies, waits for them, and re-layouts  2.16 us (2%)
    pallas_call x1, Pallas kernels, local(): pl.pallas_call(kernel, out_shape=jax.ShapeDtypeStruct((rows, width), BF16...  139 us

profile of v4, /device:TPU:1, one launch (start us, length us, event | category | flops | bytes accessed | tf_op | source)
XLA Modules:
  0.0 140.9 jit_solution(15510528933446683051)
XLA Ops:
  0.0 138.8 %moe.1 = bf16[256,1792]{1,0:T(8,128)(2,1)} custom-call(bf16[256,1792]{1,0:T(8,128)(2,1)} %refs_0_.1, bf16[1792]{0:T(1024)(128)(2,1)} %refs_1_.1, s32[8,256]{1,0:T(8,128)} %bitcast.8, bf16[8,256]{1,0:T(8,128)(2,1)} %bitcast.9, bf16[7168,512]{1,0:T(8,128)(2,1)} %bitcast.5, bf16[7168,512]{1,0:T(8,128)(2,1)} %bitcast.6, bf16[512,7168]{1,0:T(8,128)(2,1)} %bitcast.7), custom_call_target="tpu_custom_call" | custom-call | tf_op jit(solution)/shard_map/moe/pallas_call | solution.py:759
  138.8 2.2 %copy.9 = bf16[256,1792]{1,0:T(8,128)(2,1)} copy(bf16[256,1792]{1,0:T(8,128)(2,1)} %moe.1) | data formatting | bytes 1835008
